TPU v7x, 256 devices: a whole 4x4x8 slice. The times are simulated.
256 devices in a mesh: section: 8 (over z), dp: 32 (over x, y, core).
Axes of the slice: x: 4, y: 4, z: 8, core: 2. Of those that a mesh axis runs over, the one named last changes fastest.
Arguments:
- inject: bfloat16 [8, 256, 4096], P('section', 'dp'), may hold values from -42 to 42, as said below
- w_gate: bfloat16 [8, 4096, 11008], P('section', None, 'dp'), may hold values from -0.09375 to 0.09375
- w_up: bfloat16 [8, 4096, 11008], P('section', None, 'dp'), may hold values from -0.09375 to 0.09375
- w_down: bfloat16 [8, 11008, 4096], P('section', 'dp'), may hold values from -0.0546875 to 0.0546875
- gain: float32 [8, 4096], P('section'), may hold values from 0.5 to 1.5
Outputs:
- iterate: float32 [8, 256, 4096], P('section', 'dp')
- mixing: float32 [8, 5, 5], P('section')
Inputs may be any that keep to these rules, and one draw needn't show every extreme that they name: inject has entries of varied magnitude from token to token.
All inputs are finite; a program needn't handle non-finite values.
Results may differ from a plain program's by a relative error of at most 0.0038.
Values may be sent and summed in bfloat16 or wider, within the bound.
A program may use at most 64 MiB of HBM per device.

v0:
```python
import jax
import jax.numpy as jnp
from jax import lax
from jax.sharding import PartitionSpec as P

ITERS = 5
HIST = 5


def in_order(tiles, dim):
    tiles = jnp.moveaxis(tiles, 0, dim)
    dims = tiles.shape
    return tiles.reshape(*dims[:dim], dims[dim] * dims[dim + 1], *dims[dim + 2 :])


def copy_for_each(array, axis):
    peers = lax.axis_size(axis)
    return lax.all_to_all(
        jnp.broadcast_to(array[None], (peers, *array.shape)), axis, 0, 0, tiled=True
    )


def collect(array, axis, dim):
    return in_order(copy_for_each(array, axis), dim)


def split_up(array, dim, peers):
    dims = array.shape
    tiles = array.reshape(*dims[:dim], peers, dims[dim] // peers, *dims[dim + 1 :])
    return jnp.moveaxis(tiles, dim, 0)


def sent_and_summed(array, axis, dim):
    peers = lax.axis_size(axis)
    tiles = lax.all_to_all(split_up(array, dim, peers), axis, 0, 0, tiled=True)
    return jnp.sum(tiles.astype(jnp.float32), axis=0)


def passed_along(array, axis, by):
    peers = lax.axis_size(axis)
    return lax.ppermute(array, axis, [(i, (i + by) % peers) for i in range(peers)])


def of_everyone(array, axis):
    return copy_for_each(array, axis).sum(axis=0)


def rms_scaled(values, gain_row):
    inverse = lax.rsqrt(jnp.mean(values * values, axis=-1, keepdims=True) + 1e-06)
    return (values * inverse * gain_row).astype(jnp.bfloat16)


def solve_small(system, target):
    count = system.shape[-1]
    entries = [[system[..., i, j] for j in range(count)] for i in range(count)]
    values = [target[..., i] for i in range(count)]
    for p in range(count):
        for i in range(p + 1, count):
            factor = entries[i][p] / entries[p][p]
            for j in range(p, count):
                entries[i][j] = entries[i][j] - factor * entries[p][j]
            values[i] = values[i] - factor * values[p]
    answer = [None] * count
    for i in range(count - 1, -1, -1):
        accum = values[i]
        for j in range(i + 1, count):
            accum = accum - entries[i][j] * answer[j]
        answer[i] = accum / entries[i][i]
    return jnp.stack(answer, axis=-1)


def mixing_weights(matrix, iteration):
    live = (jnp.arange(HIST) <= iteration).astype(jnp.float32)
    damp = 0.01 * jnp.trace(matrix) / (iteration + 1) + 1e-06
    eye_mat = jnp.eye(HIST, dtype=jnp.float32)
    diagonal = live * damp + (1.0 - live)
    system = matrix * live[:, None] * live[None, :] + eye_mat * diagonal[None, :]
    beta = solve_small(system, live)
    return beta / jnp.sum(beta)


def local(inject, w_gate, w_up, w_down, gain):
    tok_rows = inject.shape[1]
    features = inject.shape[2]
    groups = lax.axis_size("dp")
    cell_count = float(tok_rows * groups * features)
    source = inject[0].astype(jnp.float32)
    gain_row = gain[0]
    gate_local = w_gate[0]
    up_local = w_up[0]
    down_local = w_down[0]
    iterate = jnp.zeros((tok_rows, features), jnp.float32)
    images = jnp.zeros((HIST, tok_rows, features), jnp.float32)
    misfits = jnp.zeros((HIST, tok_rows, features), jnp.float32)
    gram_matrix = jnp.zeros((HIST, HIST), jnp.float32)
    mixing = jnp.zeros((ITERS, HIST), jnp.float32)
    for iteration in range(ITERS):
        normed = rms_scaled(iterate, gain_row)
        segment = collect(normed, "dp", 0)
        gate_val = jnp.dot(segment, gate_local, preferred_element_type=jnp.float32)
        up_val = jnp.dot(segment, up_local, preferred_element_type=jnp.float32)
        hidden = (jax.nn.silu(gate_val) * up_val).astype(jnp.bfloat16)
        partials = jnp.dot(hidden, down_local, preferred_element_type=jnp.float32)
        summed = sent_and_summed(partials.astype(jnp.bfloat16), "dp", 0)
        output = (iterate + summed).astype(jnp.bfloat16)
        before = passed_along(output, "section", 1)
        mapped = source + 0.5 * before.astype(jnp.float32)
        misfit = mapped - iterate
        images = images.at[iteration].set(mapped)
        misfits = misfits.at[iteration].set(misfit)
        local_gram = (
            jnp.einsum("htd,gtd->hg", misfits, misfits, precision=lax.Precision.HIGHEST)
            / cell_count
        )
        gram_matrix = of_everyone(local_gram, "dp")
        weights = mixing_weights(gram_matrix, iteration)
        mixing = mixing.at[iteration].set(weights)
        iterate = jnp.einsum("h,htd->td", weights, images, precision=lax.Precision.HIGHEST)
    return (iterate[None], mixing[None])


def solution(mesh):
    placed = (
        P("section", "dp", None),
        P("section", None, "dp"),
        P("section", None, "dp"),
        P("section", "dp", None),
        P("section", None),
    )
    return jax.shard_map(
        local,
        mesh=mesh,
        in_specs=placed,
        out_specs=(P("section", "dp", None), P("section", None, None)),
        check_vma=False,
    )
```

profile of v0, /device:TPU:1, one launch (start us, length us, event | category | flops | bytes accessed | tf_op | source)
XLA Modules:
  0.0 711.8 jit_solution(1392657259811600408)
XLA Ops:
  1.8 36.8 %all_to_all.75 = bf16[32,8,4096]{2,1,0:T(8,128)(2,1)S(1)} all-to-all(bf16[32,8,4096]{2,1,0:T(8,128)(2,1)S(1)} %broadcast_in_dim.24), channel_id=1, replica_groups=mesh['section'=8,'dp'=32] {'dp'}, dimensions={0} | all-to-all | bytes 4194304 | tf_op jit(solution)/shard_map/all_to_all | solution.py:18
  40.9 7.4 %fusion = bf16[32,8,4096]{2,1,0:T(8,128)(2,1)} fusion(bf16[1,344,4096]{2,1,0:T(8,128)(2,1)S(1)} %copy-done, bf16[1,4096,344]{1,2,0:T(8,128)(2,1)} %param.37, bf16[32,8,4096]{2,1,0:T(8,128)(2,1)} %copy-done.2, f32[256,344]{0,1:T(8,128)S(1)} %fusion.28), kind=kOutput, calls=%fused_computation.5 | convolution fusion | flops 1444417536 | bytes 10182656 | tf_op jit(solution)/shard_map/dot_general | solution.py:103
  48.3 32.7 %all_to_all.76 = bf16[32,8,4096]{2,1,0:T(8,128)(2,1)} all-to-all(bf16[32,8,4096]{2,1,0:T(8,128)(2,1)} %fusion), channel_id=1, replica_groups=mesh['section'=8,'dp'=32] {'dp'}, dimensions={0} | all-to-all | bytes 4194304 | tf_op jit(solution)/shard_map/all_to_all | solution.py:35
  84.7 6.3 collective-permute-done
  99.0 7.1 all-to-all-done.2
  145.3 32.5 %all_to_all.77 = bf16[32,8,4096]{2,1,0:T(8,128)(2,1)S(1)} all-to-all(bf16[32,8,4096]{2,1,0:T(8,128)(2,1)S(1)} %broadcast_in_dim.26), channel_id=1, replica_groups=mesh['section'=8,'dp'=32] {'dp'}, dimensions={0} | all-to-all | bytes 4194304 | tf_op jit(solution)/shard_map/all_to_all | solution.py:18
  180.9 7.4 %fusion.1 = bf16[32,8,4096]{2,1,0:T(8,128)(2,1)} fusion(bf16[1,344,4096]{2,1,0:T(8,128)(2,1)S(1)} %copy-done, bf16[1,4096,344]{1,2,0:T(8,128)(2,1)} %param.37, bf16[32,8,4096]{2,1,0:T(8,128)(2,1)} %copy-done.3, f32[256,344]{0,1:T(8,128)} %fusion.26), kind=kOutput, calls=%fused_computation.6 | convolution fusion | flops 1444417536 | bytes 10182656 | tf_op jit(solution)/shard_map/dot_general | solution.py:103
  188.3 32.1 %all_to_all.78 = bf16[32,8,4096]{2,1,0:T(8,128)(2,1)S(1)} all-to-all(bf16[32,8,4096]{2,1,0:T(8,128)(2,1)} %fusion.1), channel_id=1, replica_groups=mesh['section'=8,'dp'=32] {'dp'}, dimensions={0} | all-to-all | bytes 4194304 | tf_op jit(solution)/shard_map/all_to_all | solution.py:35
  234.0 4.6 all-to-all-start.5
  285.8 32.5 %all_to_all.79 = bf16[32,8,4096]{2,1,0:T(8,128)(2,1)S(1)} all-to-all(bf16[32,8,4096]{2,1,0:T(8,128)(2,1)S(1)} %broadcast_in_dim.28), channel_id=1, replica_groups=mesh['section'=8,'dp'=32] {'dp'}, dimensions={0} | all-to-all | bytes 4194304 | tf_op jit(solution)/shard_map/all_to_all | solution.py:18
  321.4 7.4 %fusion.2 = bf16[32,8,4096]{2,1,0:T(8,128)(2,1)} fusion(bf16[1,344,4096]{2,1,0:T(8,128)(2,1)S(1)} %copy-done, bf16[1,4096,344]{1,2,0:T(8,128)(2,1)} %param.37, bf16[32,8,4096]{2,1,0:T(8,128)(2,1)} %copy-done.4, f32[256,344]{0,1:T(8,128)} %fusion.24), kind=kOutput, calls=%fused_computation.7 | convolution fusion | flops 1444417536 | bytes 10182656 | tf_op jit(solution)/shard_map/dot_general | solution.py:103
  328.8 32.1 %all_to_all.80 = bf16[32,8,4096]{2,1,0:T(8,128)(2,1)S(1)} all-to-all(bf16[32,8,4096]{2,1,0:T(8,128)(2,1)} %fusion.2), channel_id=1, replica_groups=mesh['section'=8,'dp'=32] {'dp'}, dimensions={0} | all-to-all | bytes 4194304 | tf_op jit(solution)/shard_map/all_to_all | solution.py:35
  361.3 4.7 collective-permute-done.2
  374.6 4.6 all-to-all-start.8
  426.3 32.5 %all_to_all.81 = bf16[32,8,4096]{2,1,0:T(8,128)(2,1)S(1)} all-to-all(bf16[32,8,4096]{2,1,0:T(8,128)(2,1)S(1)} %broadcast_in_dim.30), channel_id=1, replica_groups=mesh['section'=8,'dp'=32] {'dp'}, dimensions={0} | all-to-all | bytes 4194304 | tf_op jit(solution)/shard_map/all_to_all | solution.py:18
  462.0 7.4 %fusion.3 = bf16[32,8,4096]{2,1,0:T(8,128)(2,1)} fusion(bf16[1,344,4096]{2,1,0:T(8,128)(2,1)S(1)} %copy-done, bf16[1,4096,344]{1,2,0:T(8,128)(2,1)} %param.37, bf16[32,8,4096]{2,1,0:T(8,128)(2,1)} %copy-done.5, f32[256,344]{0,1:T(8,128)} %fusion.22), kind=kOutput, calls=%fused_computation.8 | convolution fusion | flops 1444417536 | bytes 10182656 | tf_op jit(solution)/shard_map/dot_general | solution.py:103
  469.4 32.1 %all_to_all.82 = bf16[32,8,4096]{2,1,0:T(8,128)(2,1)S(1)} all-to-all(bf16[32,8,4096]{2,1,0:T(8,128)(2,1)} %fusion.3), channel_id=1, replica_groups=mesh['section'=8,'dp'=32] {'dp'}, dimensions={0} | all-to-all | bytes 4194304 | tf_op jit(solution)/shard_map/all_to_all | solution.py:35
  501.9 4.7 collective-permute-done.3
  515.1 4.6 all-to-all-start.11
  567.4 32.5 %all_to_all.83 = bf16[32,8,4096]{2,1,0:T(8,128)(2,1)S(1)} all-to-all(bf16[32,8,4096]{2,1,0:T(8,128)(2,1)S(1)} %broadcast_in_dim.32), channel_id=1, replica_groups=mesh['section'=8,'dp'=32] {'dp'}, dimensions={0} | all-to-all | bytes 4194304 | tf_op jit(solution)/shard_map/all_to_all | solution.py:18
  602.3 7.4 %fusion.4 = bf16[32,8,4096]{2,1,0:T(8,128)(2,1)} fusion(bf16[1,344,4096]{2,1,0:T(8,128)(2,1)S(1)} %copy-done, bf16[1,4096,344]{1,2,0:T(8,128)(2,1)} %param.37, bf16[32,8,4096]{2,1,0:T(8,128)(2,1)} %copy-done.6, f32[256,344]{0,1:T(8,128)S(1)} %fusion.20), kind=kOutput, calls=%fused_computation.9 | convolution fusion | flops 1444417536 | bytes 10182656 | tf_op jit(solution)/shard_map/dot_general | solution.py:103
  609.7 4.5 all-to-all-start.13
  615.3 27.4 %all-to-all-done.13 = bf16[32,8,4096]{2,1,0:T(8,128)(2,1)} async-done(((bf16[32,8,4096]{2,1,0:T(8,128)(2,1)}), bf16[32,8,4096]{2,1,0:T(8,128)(2,1)}, u32[]{:S(2)}, u32[]{:S(2)}) %all-to-all-start.13) | async-done | bytes 2097184 | tf_op jit(solution)/shard_map/all_to_all | solution.py:35
  657.6 5.5 all-to-all-start.14
  (173 shorter events, 129.3 us)
Async XLA Ops:
  0.6 40.3 %copy-start = (bf16[1,344,4096]{2,1,0:T(8,128)(2,1)S(1)}, bf16[1,344,4096]{2,1,0:T(8,128)(2,1)}, u32[]{:S(2)}) copy-start(bf16[1,344,4096]{2,1,0:T(8,128)(2,1)} %param.38) | copy-start | bytes 8454148
  1.8 38.1 %copy-start.9 = (bf16[1,4096,344]{1,2,0:T(8,128)(2,1)S(1)}, bf16[1,4096,344]{1,2,0:T(8,128)(2,1)}, u32[]{:S(2)}) copy-start(bf16[1,4096,344]{1,2,0:T(8,128)(2,1)} %param.36) | copy-start | bytes 8454148
  38.6 1.3 copy-start.2
  81.1 9.9 %copy-start.7 = (bf16[1,8,4096]{2,1,0:T(8,128)(2,1)S(1)}, bf16[1,8,4096]{2,1,0:T(8,128)(2,1)}, u32[]{:S(2)}) copy-start(bf16[1,8,4096]{2,1,0:T(8,128)(2,1)} %param.35) | copy-start | bytes 196612
  81.1 63.9 %copy-start.8 = (f32[1,4096]{1,0:T(1,128)S(1)}, f32[1,4096]{1,0:T(1,128)}, u32[]{:S(2)}) copy-start(f32[1,4096]{1,0:T(1,128)} %param.39) | copy-start | bytes 49156
  83.0 8.0 %collective-permute-start = (bf16[8,4096]{1,0:T(8,128)(2,1)S(1)}, bf16[8,4096]{1,0:T(8,128)(2,1)S(1)}, u32[]{:S(2)}, u32[]{:S(2)}) collective-permute-start(bf16[8,4096]{1,0:T(8,128)(2,1)S(1)} %reduce_sum.247), channel_id=1, source_target_pairs={{0,32},{32,64},{64,96},{96,128},{128,160},{160,192},{192,224},{224... | collective-permute-start | bytes 196616 | tf_op jit(solution)/shard_map/ppermute | solution.py:41
  94.2 12.0 %all-to-all-start.2 = ((f32[32,5,5]{2,1,0:T(8,128)}), f32[32,5,5]{2,1,0:T(8,128)S(1)}, u32[]{:S(2)}, u32[]{:S(2)}) async-start(f32[32,5,5]{2,1,0:T(8,128)} %broadcast_in_dim.25), calls=%async_computation.2 | async-start | bytes 262144 | tf_op jit(solution)/shard_map/all_to_all | solution.py:18
  145.3 33.8 %copy-start.10 = (bf16[1,4096,344]{1,2,0:T(8,128)(2,1)S(1)}, bf16[1,4096,344]{1,2,0:T(8,128)(2,1)}, u32[]{:S(2)}) copy-start(bf16[1,4096,344]{1,2,0:T(8,128)(2,1)} %param.36) | copy-start | bytes 8454148
  177.8 1.4 copy-start.3
  220.7 4.8 collective-permute-start.1
  234.0 12.3 %all-to-all-start.5 = ((f32[32,5,5]{2,1,0:T(8,128)}), f32[32,5,5]{2,1,0:T(8,128)S(1)}, u32[]{:S(2)}, u32[]{:S(2)}) async-start(f32[32,5,5]{2,1,0:T(8,128)} %broadcast_in_dim.27), calls=%async_computation.5 | async-start | bytes 262144 | tf_op jit(solution)/shard_map/all_to_all | solution.py:18
  285.8 33.8 %copy-start.11 = (bf16[1,4096,344]{1,2,0:T(8,128)(2,1)S(1)}, bf16[1,4096,344]{1,2,0:T(8,128)(2,1)}, u32[]{:S(2)}) copy-start(bf16[1,4096,344]{1,2,0:T(8,128)(2,1)} %param.36) | copy-start | bytes 8454148
  318.3 1.4 copy-start.4
  361.2 4.8 collective-permute-start.2
  374.6 12.3 %all-to-all-start.8 = ((f32[32,5,5]{2,1,0:T(8,128)}), f32[32,5,5]{2,1,0:T(8,128)S(1)}, u32[]{:S(2)}, u32[]{:S(2)}) async-start(f32[32,5,5]{2,1,0:T(8,128)} %broadcast_in_dim.29), calls=%async_computation.8 | async-start | bytes 262144 | tf_op jit(solution)/shard_map/all_to_all | solution.py:18
  426.3 33.9 %copy-start.12 = (bf16[1,4096,344]{1,2,0:T(8,128)(2,1)S(1)}, bf16[1,4096,344]{1,2,0:T(8,128)(2,1)}, u32[]{:S(2)}) copy-start(bf16[1,4096,344]{1,2,0:T(8,128)(2,1)} %param.36) | copy-start | bytes 8454148
  458.8 1.4 copy-start.5
  501.8 4.8 collective-permute-start.3
  515.1 12.3 %all-to-all-start.11 = ((f32[32,5,5]{2,1,0:T(8,128)}), f32[32,5,5]{2,1,0:T(8,128)S(1)}, u32[]{:S(2)}, u32[]{:S(2)}) async-start(f32[32,5,5]{2,1,0:T(8,128)} %broadcast_in_dim.31), calls=%async_computation.11 | async-start | bytes 262144 | tf_op jit(solution)/shard_map/all_to_all | solution.py:18
  567.4 33.8 %copy-start.13 = (bf16[1,4096,344]{1,2,0:T(8,128)(2,1)S(1)}, bf16[1,4096,344]{1,2,0:T(8,128)(2,1)}, u32[]{:S(2)}) copy-start(bf16[1,4096,344]{1,2,0:T(8,128)(2,1)} %param.36) | copy-start | bytes 8454148
  600.0 1.3 copy-start.6
  609.7 33.0 %all-to-all-start.13 = ((bf16[32,8,4096]{2,1,0:T(8,128)(2,1)}), bf16[32,8,4096]{2,1,0:T(8,128)(2,1)}, u32[]{:S(2)}, u32[]{:S(2)}) async-start(bf16[32,8,4096]{2,1,0:T(8,128)(2,1)} %fusion.4), calls=%async_computation.13 | async-start | bytes 4194304 | tf_op jit(solution)/shard_map/all_to_all | solution.py:35
  644.7 4.4 collective-permute-start.4
  657.6 13.3 %all-to-all-start.14 = ((f32[32,5,5]{2,1,0:T(8,128)}), f32[32,5,5]{2,1,0:T(8,128)S(1)}, u32[]{:S(2)}, u32[]{:S(2)}) async-start(f32[32,5,5]{2,1,0:T(8,128)} %broadcast_in_dim.33), calls=%async_computation.14 | async-start | bytes 262144 | tf_op jit(solution)/shard_map/all_to_all | solution.py:18
  (1 other events, 1.0 us)
where the time goes:
time: 724 us; the launch traced here: 712 us
  blocking collectives  296 us (41%)
  between operations  176 us (24%)
  matrix products  72.7 us (10%)
  waiting for transfers between devices  71.1 us (10%)
  local copies, waits for them, and re-layouts  55.4 us (8%)
  starting transfers between devices  30.2 us (4%)
  other arithmetic  11.1 us (2%)
    all_to_all x5, blocking collectives, copy_for_each(): lax.all_to_all(jnp.broadcast_to(array[None], (peers, *array.shape)), axis...  167 us
    all_to_all x4, blocking collectives, sent_and_summed(): tiles = lax.all_to_all(split_up(array, dim, peers), axis, 0, 0, tiled=True)  129 us
    dot_general x5, matrix products, local(): partials = jnp.dot(hidden, down_local, preferred_element_type=jnp.float32)  37 us
    all_to_all x1, waiting for transfers between devices, sent_and_summed(): tiles = lax.all_to_all(split_up(array, dim, peers), axis, 0, 0, tiled=True)  27.4 us
    all_to_all x5, starting transfers between devices, copy_for_each(): lax.all_to_all(jnp.broadcast_to(array[None], (peers, *array.shape)), axis...  23.6 us
    ppermute x5, waiting for transfers between devices, passed_along(): lax.ppermute(array, axis, [(i, (i + by) % peers) for i in range(peers)])  22.6 us
    all_to_all x5, waiting for transfers between devices, copy_for_each(): lax.all_to_all(jnp.broadcast_to(array[None], (peers, *array.shape)), axis...  21.2 us
    dot_general x5, matrix products, local(): jnp.einsum('htd,gtd->hg', misfits, misfits, precision=lax.Precision.HIGHEST)  18.4 us
  transfers between devices with their start and end apart: 11, of which 11 were waited for; matrix products, arithmetic and copies ran while one was open for 3% of the time, Pallas kernels for 0%

commit v1 on v0

v1 whole, which is shorter than its diff:
```python
import jax
import jax.numpy as jnp
from jax import lax
from jax.experimental import pallas as pl
from jax.experimental.pallas import tpu as pltpu
from jax.sharding import PartitionSpec as P

ITERS = 5
HIST = 5
SECTIONS = 8
RING = 4
N_DP = 32
ROWS = 8
PACK = RING * ROWS
TOK = RING * PACK
D = 4096
FFL = 344
FFP = 384
CHUNKS = 4
CH = D // CHUNKS
NT = 512
MESH = pl.DeviceIdType.MESH
F32 = jnp.float32
BF16 = jnp.bfloat16


def solve_small(entries, values):
    count = len(values)
    entries = [list(row) for row in entries]
    values = list(values)
    for p in range(count):
        for i in range(p + 1, count):
            factor = entries[i][p] / entries[p][p]
            for j in range(p, count):
                entries[i][j] = entries[i][j] - factor * entries[p][j]
            values[i] = values[i] - factor * values[p]
    answer = [None] * count
    for i in range(count - 1, -1, -1):
        accum = values[i]
        for j in range(i + 1, count):
            accum = accum - entries[i][j] * answer[j]
        answer[i] = accum / entries[i][i]
    return answer


def kernel(
    inject_ref, gain_ref, wg_hbm, wu_hbm, wd_hbm,
    iterate_ref, mixing_ref,
    wgu, wd, acc, hid, images, misfits, x_ref,
    nsend, nrecv, g, p, pr, q, qown, qr, osend, orecv, gmsg, grecv, gram_s,
    w_local, w_send, w_recv,
    as_send, as_recv, ab_send, ab_recv, rb_send, rb_recv, rs_send, rs_recv,
    z_send, z_recv, g_send, g_recv,
):
    sec = lax.axis_index("section")
    dp = lax.axis_index("dp")
    core = lax.rem(dp, 2)
    cx = lax.div(dp, 8)
    cy = lax.rem(lax.div(dp, 2), RING)
    small = cx + core * (cy - cx)
    big = cy + core * (cx - cy)
    step_small = 8 - 6 * core
    step_big = 2 + 6 * core

    def at_small(j):
        return (sec, lax.rem(small + RING + j, RING) * step_small + big * step_big + core)

    def at_big(j):
        return (sec, small * step_small + lax.rem(big + RING + j, RING) * step_big + core)

    sibling = (sec, dp + 1 - 2 * core)
    after = (lax.rem(sec + 1, SECTIONS), dp)
    before = (lax.rem(sec + SECTIONS - 1, SECTIONS), dp)

    def remote(src, dst, send, recv, device):
        return pltpu.make_async_remote_copy(
            src_ref=src, dst_ref=dst, send_sem=send, recv_sem=recv, device_id=device, device_id_type=MESH
        )

    local_copies = [
        pltpu.make_async_copy(wg_hbm, wgu.at[pl.ds(0, FFL), :], w_local.at[0]),
        pltpu.make_async_copy(wu_hbm, wgu.at[pl.ds(2 * FFP, FFL), :], w_local.at[1]),
        pltpu.make_async_copy(wd_hbm, wd.at[pl.ds(0, FFL), :], w_local.at[2]),
    ]
    shared_copies = [
        remote(wg_hbm, wgu.at[pl.ds(FFP, FFL), :], w_send.at[0], w_recv.at[0], sibling),
        remote(wu_hbm, wgu.at[pl.ds(3 * FFP, FFL), :], w_send.at[1], w_recv.at[1], sibling),
        remote(wd_hbm, wd.at[pl.ds(FFP, FFL), :], w_send.at[2], w_recv.at[2], sibling),
    ]
    for copy in local_copies:
        copy.start()

    barrier = pltpu.get_barrier_semaphore()

    @pl.loop(1, N_DP)
    def _(d):
        pl.semaphore_signal(barrier, inc=1, device_id=(sec, lax.rem(dp + d, N_DP)), device_id_type=MESH)

    pl.semaphore_signal(barrier, inc=1, device_id=after, device_id_type=MESH)
    pl.semaphore_signal(barrier, inc=1, device_id=before, device_id_type=MESH)

    x_ref[...] = jnp.zeros_like(x_ref)
    images[...] = jnp.zeros_like(images)
    misfits[...] = jnp.zeros_like(misfits)
    gram_s[...] = jnp.zeros_like(gram_s)
    for h in range(2):
        wd[h * FFP + FFL : (h + 1) * FFP, :] = jnp.zeros((FFP - FFL, D), BF16)

    pl.semaphore_wait(barrier, N_DP + 1)
    for copy in shared_copies:
        copy.start()

    lane = lax.broadcasted_iota(jnp.int32, (1, 128), 1)
    cells = float(ROWS * N_DP * D)

    def cols(c):
        return pl.ds(c * CH, CH)

    def small_gather(c, j):
        return remote(
            nsend.at[:, cols(c)], nrecv.at[j - 1, :, cols(c)], as_send.at[c, j - 1], as_recv.at[c, j - 1], at_small(j)
        )

    def big_gather(c, j):
        return remote(
            g.at[0, :, cols(c)], g.at[j, :, cols(c)], ab_send.at[c, j - 1], ab_recv.at[c, j - 1], at_big(j)
        )

    def big_reduce(c, j):
        return remote(
            p.at[j, :, cols(c)], pr.at[j - 1, :, cols(c)], rb_send.at[c, j - 1], rb_recv.at[c, j - 1], at_big(-j)
        )

    def small_reduce(c, j):
        return remote(
            q.at[j - 1, :, cols(c)], qr.at[j - 1, :, cols(c)], rs_send.at[c, j - 1], rs_recv.at[c, j - 1], at_small(-j)
        )

    @pl.loop(0, ITERS)
    def _(k):
        parity = lax.rem(k, 2)

        def relay(c):
            return remote(
                osend.at[:, cols(c)], orecv.at[k, :, cols(c)], z_send.at[c], z_recv.at[k, c], after
            )

        x = x_ref[...]
        inverse = lax.rsqrt(jnp.mean(x * x, axis=-1, keepdims=True) + 1e-06)
        for c in range(CHUNKS):
            nsend[:, cols(c)] = (x_ref[:, cols(c)] * inverse * gain_ref[:, cols(c)]).astype(BF16)

        @pl.when(k > 0)
        def _():
            for c in range(CHUNKS):
                for j in (1, 3, 2):
                    small_gather(c, j).start()
            for c in range(CHUNKS):
                for j in (1, 3, 2):
                    small_gather(c, j).wait_recv()
                rows = [nsend[:, cols(c)].astype(F32)] + [nrecv[j, :, cols(c)].astype(F32) for j in range(3)]
                g[0, :, cols(c)] = jnp.concatenate(rows, axis=0).astype(BF16)
                for j in (1, 3, 2):
                    big_gather(c, j).start()

        @pl.when(k == 0)
        def _():
            for c in range(CHUNKS):
                mine = nsend[:, cols(c)].astype(F32)
                packed = jnp.concatenate([mine] * RING, axis=0).astype(BF16)
                for j in range(RING):
                    g[j, :, cols(c)] = packed
            for copy in local_copies:
                copy.wait()
            for copy in shared_copies:
                copy.wait_recv()

        for c in range(CHUNKS):
            @pl.when(k > 0)
            def _():
                for j in (1, 3, 2):
                    big_gather(c, j).wait_recv()

            tokens = g[:, :, cols(c)].reshape(TOK, CH)

            @pl.loop(0, 4 * FFP // NT)
            def _(n):
                at = pl.ds(pl.multiple_of(n * NT, NT), NT)
                product = lax.dot_general(
                    tokens, wgu[at, cols(c)], (((1,), (1,)), ((), ())), preferred_element_type=F32
                )
                if c == 0:
                    acc[:, at] = product
                else:
                    acc[:, at] += product

        for h in range(2):
            gate = acc[:, h * FFP : (h + 1) * FFP]
            up = acc[:, (2 + h) * FFP : (3 + h) * FFP]
            value = gate / (1.0 + jnp.exp(-gate)) * up
            real = lax.broadcasted_iota(jnp.int32, (TOK, FFP), 1) < FFL
            hid[:, h * FFP : (h + 1) * FFP] = jnp.where(real, value, 0.0).astype(BF16)

        for c in range(CHUNKS):
            product = jnp.dot(hid[...], wd[:, cols(c)], preferred_element_type=F32).astype(BF16)
            p[:, :, cols(c)] = product.reshape(RING, PACK, CH)
            for j in (1, 3, 2):
                big_reduce(c, j).start()

        for c in range(CHUNKS):
            for j in (1, 3, 2):
                big_reduce(c, j).wait_recv()
            total = p[0, :, cols(c)].astype(F32)
            for j in range(3):
                total = total + pr[j, :, cols(c)].astype(F32)
            qown[:, cols(c)] = total[:ROWS]
            for j in (1, 3, 2):
                q[j - 1, :, cols(c)] = total[j * ROWS : (j + 1) * ROWS].astype(BF16)
                small_reduce(c, j).start()

        for c in range(CHUNKS):
            for j in (1, 3, 2):
                small_reduce(c, j).wait_recv()
            total = qown[:, cols(c)]
            for j in range(3):
                total = total + qr[j, :, cols(c)].astype(F32)
            osend[:, cols(c)] = (x_ref[:, cols(c)] + total).astype(BF16)
            relay(c).start()

        sums = [jnp.zeros((ROWS, CH), F32) for _ in range(HIST)]
        for c in range(CHUNKS):
            relay(c).wait_recv()
            mapped = inject_ref[:, cols(c)].astype(F32) + 0.5 * orecv[k, :, cols(c)].astype(F32)
            misfit = mapped - x_ref[:, cols(c)]
            images[k, :, cols(c)] = mapped
            misfits[k, :, cols(c)] = misfit
            sums = [sums[i] + misfit * misfits[i, :, cols(c)] for i in range(HIST)]
        row = jnp.zeros((1, 128), F32)
        for i in range(HIST):
            value = jnp.sum(jnp.sum(sums[i], axis=0, keepdims=True), axis=1, keepdims=True)
            row = jnp.where(lane == i, value, row)
        gmsg[...] = row

        @pl.loop(1, N_DP)
        def _(d):
            remote(
                gmsg, grecv.at[parity, d - 1], g_send, g_recv.at[parity], (sec, lax.rem(dp + d, N_DP))
            ).start()

        @pl.when(k > 0)
        def _():
            for c in range(CHUNKS):
                for j in (1, 3, 2):
                    small_gather(c, j).wait_send()
                    big_gather(c, j).wait_send()
        for c in range(CHUNKS):
            for j in (1, 3, 2):
                big_reduce(c, j).wait_send()
                small_reduce(c, j).wait_send()
            relay(c).wait_send()
        pltpu.make_async_copy(grecv.at[parity], grecv.at[parity], g_recv.at[parity]).wait()
        row = (row + jnp.sum(grecv[parity], axis=0)) / cells
        pltpu.make_async_copy(grecv.at[parity], grecv.at[parity], g_send).wait()

        fresh = [
            jnp.broadcast_to(jnp.sum(jnp.where(lane == i, row, 0.0), axis=1, keepdims=True), (8, 128))
            for i in range(HIST)
        ]
        gram = [[None] * HIST for _ in range(HIST)]
        for i in range(HIST):
            for j in range(i + 1):
                slot = i * (i + 1) // 2 + j
                entry = jnp.where(k == i, fresh[j], gram_s[slot])
                gram_s[slot] = entry
                gram[i][j] = entry
                gram[j][i] = entry
        steps = jnp.full((8, 128), k + 1, jnp.int32)
        live = [jnp.where(steps > i, 1.0, 0.0) for i in range(HIST)]
        trace = gram[0][0]
        for i in range(1, HIST):
            trace = trace + gram[i][i]
        damp = 0.01 * trace / steps.astype(F32) + 1e-06
        system = [[gram[i][j] * live[i] * live[j] for j in range(HIST)] for i in range(HIST)]
        for i in range(HIST):
            system[i][i] = system[i][i] + (live[i] * damp + (1.0 - live[i]))
        beta = solve_small(system, live)
        whole = beta[0]
        for i in range(1, HIST):
            whole = whole + beta[i]
        weights = [value / whole for value in beta]
        mixed = jnp.zeros((1, 128), F32)
        for i in range(HIST):
            mixed = jnp.where(lane == i, weights[i][:1], mixed)
        mixing_ref[pl.ds(k, 1), :] = mixed[:, :HIST]
        for c in range(D // 128):
            at = pl.ds(c * 128, 128)
            value = weights[0] * images[0, :, at]
            for i in range(1, HIST):
                value = value + weights[i] * images[i, :, at]
            x_ref[:, at] = value

    for copy in shared_copies:
        copy.wait_send()
    iterate_ref[...] = x_ref[...]


def local(inject, w_gate, w_up, w_down, gain):
    vmem = pl.BlockSpec(memory_space=pltpu.VMEM)
    hbm = pl.BlockSpec(memory_space=pl.ANY)
    dma = pltpu.SemaphoreType.DMA
    iterate, mixing = pl.pallas_call(
        kernel,
        out_shape=(jax.ShapeDtypeStruct((ROWS, D), F32), jax.ShapeDtypeStruct((ITERS, HIST), F32)),
        in_specs=[vmem, vmem, hbm, hbm, hbm],
        out_specs=(vmem, vmem),
        scratch_shapes=[
            pltpu.VMEM((4 * FFP, D), BF16),
            pltpu.VMEM((2 * FFP, D), BF16),
            pltpu.VMEM((TOK, 4 * FFP), F32),
            pltpu.VMEM((TOK, 2 * FFP), BF16),
            pltpu.VMEM((HIST, ROWS, D), F32),
            pltpu.VMEM((HIST, ROWS, D), F32),
            pltpu.VMEM((ROWS, D), F32),
            pltpu.VMEM((ROWS, D), BF16),
            pltpu.VMEM((3, ROWS, D), BF16),
            pltpu.VMEM((RING, PACK, D), BF16),
            pltpu.VMEM((RING, PACK, D), BF16),
            pltpu.VMEM((3, PACK, D), BF16),
            pltpu.VMEM((3, ROWS, D), BF16),
            pltpu.VMEM((ROWS, D), F32),
            pltpu.VMEM((3, ROWS, D), BF16),
            pltpu.VMEM((ROWS, D), BF16),
            pltpu.VMEM((ITERS, ROWS, D), BF16),
            pltpu.VMEM((1, 128), F32),
            pltpu.VMEM((2, N_DP - 1, 1, 128), F32),
            pltpu.VMEM((HIST * (HIST + 1) // 2, 8, 128), F32),
            dma((3,)), dma((3,)), dma((3,)),
            dma((CHUNKS, 3)), dma((CHUNKS, 3)), dma((CHUNKS, 3)), dma((CHUNKS, 3)),
            dma((CHUNKS, 3)), dma((CHUNKS, 3)), dma((CHUNKS, 3)), dma((CHUNKS, 3)),
            dma((CHUNKS,)), dma((ITERS, CHUNKS)), dma, dma((2,)),
        ],
        compiler_params=pltpu.CompilerParams(
            collective_id=0, has_side_effects=True, vmem_limit_bytes=62 * 1024 * 1024
        ),
    )(inject[0], gain, w_gate[0].T, w_up[0].T, w_down[0])
    return iterate[None], mixing[None]


def solution(mesh):
    return jax.shard_map(
        local,
        mesh=mesh,
        in_specs=(
            P("section", "dp", None),
            P("section", None, "dp"),
            P("section", None, "dp"),
            P("section", "dp", None),
            P("section", None),
        ),
        out_specs=(P("section", "dp", None), P("section", None, None)),
        check_vma=False,
    )
```

time: 724 us -> 204 us (0.28); the launches traced: 712 us -> 204 us
  blocking collectives: 296 us -> 0 us
  Pallas kernels: 0 us -> 201 us
  between operations: 176 us -> 0.64 us
  matrix products: 72.7 us -> 0 us
  waiting for transfers between devices: 71.1 us -> 0 us
  local copies, waits for them, and re-layouts: 55.4 us -> 2.83 us
  starting transfers between devices: 30.2 us -> 0 us
  other arithmetic: 11.1 us -> 0 us
    all_to_all x9 -> x0, blocking collectives: 296 us -> none  [the longest x5 167 us: copy_for_each(): lax.all_to_all(jnp.broadcast_to(array[None], (peers, *array.shape)), axis...]
    pallas_call x0 -> x1, Pallas kernels: none -> 201 us  [local(): pl.pallas_call(kernel, out_shape=(jax.ShapeDtypeStruct((ROWS, D), F32), j...]
    dot_general x20 -> x0, matrix products: 72.7 us -> none  [the longest x5 37 us: local(): partials = jnp.dot(hidden, down_local, preferred_element_type=jnp.float32)]
    all_to_all x6 -> x0, waiting for transfers between devices: 48.6 us -> none  [the longest x1 27.4 us: sent_and_summed(): tiles = lax.all_to_all(split_up(array, dim, peers), axis, 0, 0, tiled=True)]
    scatter x13 -> x0, local copies, waits for them, and re-layouts: 28.6 us -> none  [the longest x5 14.3 us: local(): misfits = misfits.at[iteration].set(misfit)]
    all_to_all x6 -> x0, starting transfers between devices: 28.2 us -> none  [the longest x5 23.6 us: copy_for_each(): lax.all_to_all(jnp.broadcast_to(array[None], (peers, *array.shape)), axis...]
    ppermute x5 -> x0, waiting for transfers between devices: 22.6 us -> none  [passed_along(): lax.ppermute(array, axis, [(i, (i + by) % peers) for i in range(peers)])]
    slice x15 -> x0, local copies, waits for them, and re-layouts: 10.2 us -> none  [the longest x10 6.87 us: solve_small(): entries = [[system[..., i, j] for j in range(count)] for i in range(count)]]
  transfers between devices with their start and end apart: 11 -> 0, of which waited for: 11 -> 0; matrix products, arithmetic and copies ran while one was open for 3% -> 0% of each run, Pallas kernels for 0% -> 0%
where the time goes in v1:
time: 204 us
  Pallas kernels  201 us (99%)
  local copies, waits for them, and re-layouts  2.83 us (1%)
    pallas_call x1, Pallas kernels, local(): pl.pallas_call(kernel, out_shape=(jax.ShapeDtypeStruct((ROWS, D), F32), j...  201 us

profile of v1, /device:TPU:1, one launch (start us, length us, event | category | flops | bytes accessed | tf_op | source)
XLA Modules:
  0.0 204.3 jit_solution(7477490646691646850)
XLA Ops:
  0.6 200.8 %shard_map.68 = (f32[8,4096]{1,0:T(8,128)}, f32[5,5]{1,0:T(8,128)}) custom-call(bf16[8,4096]{1,0:T(8,128)(2,1)} %bitcast.14, f32[1,4096]{1,0:T(1,128)} %gain_ref.1, bf16[344,4096]{1,0:T(8,128)(2,1)} %bitcast.10, bf16[344,4096]{1,0:T(8,128)(2,1)} %bitcast.11, bf16[344,4096]{1,0:T(8,128)(2,1)} %bitcast.12), custom_call_target="tpu_custom_call" | custom-call | tf_op jit(solution)/shard_map/pallas_call | solution.py:311
  201.4 1.3 copy.7
  202.7 1.6 copy.9

commit v2 on v1

--- a/solution.py
+++ b/solution.py
@@ -19,6 +19,10 @@
 CHUNKS = 4
 CH = D // CHUNKS
 NT = 512
+RELAYED = ()
+HALF = PACK // 2
+LOW = pl.ds(0, HALF)
+HIGH = pl.ds(HALF, HALF)
 MESH = pl.DeviceIdType.MESH
 F32 = jnp.float32
 BF16 = jnp.bfloat16
@@ -46,11 +50,11 @@
 def kernel(
     inject_ref, gain_ref, wg_hbm, wu_hbm, wd_hbm,
     iterate_ref, mixing_ref,
-    wgu, wd, acc, hid, images, misfits, x_ref,
-    nsend, nrecv, g, p, pr, q, qown, qr, osend, orecv, gmsg, grecv, gram_s,
+    wgu, wgt, eye, wd, pre, hid, images, misfits, x_ref, prev,
+    nsend, nrecv, g, p, ph, pr, q, qown, qr, osend, orecv, gmsg, grecv, gram_s, coef, inv_s, inv_w,
     w_local, w_send, w_recv,
     as_send, as_recv, ab_send, ab_recv, rb_send, rb_recv, rs_send, rs_recv,
-    z_send, z_recv, g_send, g_recv,
+    z_send, z_recv, g_send, g_recv, i_send, i_recv,
 ):
     sec = lax.axis_index("section")
     dp = lax.axis_index("dp")
@@ -79,14 +83,20 @@
 
     local_copies = [
         pltpu.make_async_copy(wg_hbm, wgu.at[pl.ds(0, FFL), :], w_local.at[0]),
-        pltpu.make_async_copy(wu_hbm, wgu.at[pl.ds(2 * FFP, FFL), :], w_local.at[1]),
-        pltpu.make_async_copy(wd_hbm, wd.at[pl.ds(0, FFL), :], w_local.at[2]),
+        pltpu.make_async_copy(wu_hbm, wgu.at[pl.ds(FFP, FFL), :], w_local.at[1]),
     ]
     shared_copies = [
-        remote(wg_hbm, wgu.at[pl.ds(FFP, FFL), :], w_send.at[0], w_recv.at[0], sibling),
+        remote(wg_hbm, wgu.at[pl.ds(2 * FFP, FFL), :], w_send.at[0], w_recv.at[0], sibling),
         remote(wu_hbm, wgu.at[pl.ds(3 * FFP, FFL), :], w_send.at[1], w_recv.at[1], sibling),
-        remote(wd_hbm, wd.at[pl.ds(FFP, FFL), :], w_send.at[2], w_recv.at[2], sibling),
     ]
+    for c in range(CHUNKS):
+        at = pl.ds(c * CH, CH)
+        local_copies.append(pltpu.make_async_copy(wd_hbm.at[:, at], wd.at[pl.ds(0, FFL), at], w_local.at[2 + c]))
+        shared_copies.append(
+            remote(wd_hbm.at[:, at], wd.at[pl.ds(FFP, FFL), at], w_send.at[2 + c], w_recv.at[2 + c], sibling)
+        )
+    local_copies = local_copies[2:] + local_copies[:2]
+    shared_copies = shared_copies[2:] + shared_copies[:2]
     for copy in local_copies:
         copy.start()
 
@@ -99,18 +109,35 @@
     pl.semaphore_signal(barrier, inc=1, device_id=after, device_id_type=MESH)
     pl.semaphore_signal(barrier, inc=1, device_id=before, device_id_type=MESH)
 
-    x_ref[...] = jnp.zeros_like(x_ref)
-    images[...] = jnp.zeros_like(images)
-    misfits[...] = jnp.zeros_like(misfits)
-    gram_s[...] = jnp.zeros_like(gram_s)
+    for ref in (x_ref, prev, images, misfits, gram_s, coef):
+        ref[...] = jnp.zeros_like(ref)
+    for l in range(HIST - 1):
+        pre[l] = jnp.zeros((TOK, 4 * FFP), F32)
     for h in range(2):
+        wgu[2 * h * FFP + FFL : (2 * h + 1) * FFP, :] = jnp.zeros((FFP - FFL, D), BF16)
+        wgu[(2 * h + 1) * FFP + FFL : (2 * h + 2) * FFP, :] = jnp.zeros((FFP - FFL, D), BF16)
         wd[h * FFP + FFL : (h + 1) * FFP, :] = jnp.zeros((FFP - FFL, D), BF16)
+
+    corner = lax.broadcasted_iota(jnp.int32, (256, 256), 0) == lax.broadcasted_iota(jnp.int32, (256, 256), 1)
+    eye[...] = jnp.where(corner, 1.0, 0.0).astype(BF16)
+
+    def turn(half):
+        @pl.loop(0, D // 256)
+        def _(n):
+            at = pl.ds(pl.multiple_of(n * 256, 256), 256)
+            rows = pl.ds(half * 2 * FFP, 2 * FFP)
+            wgt[at, rows] = lax.dot_general(
+                eye[...], wgu[rows, at], (((1,), (1,)), ((), ())), preferred_element_type=F32
+            ).astype(BF16)
 
     pl.semaphore_wait(barrier, N_DP + 1)
     for copy in shared_copies:
         copy.start()
 
     lane = lax.broadcasted_iota(jnp.int32, (1, 128), 1)
+    wide = lax.broadcasted_iota(jnp.int32, (ROWS, 128), 1)
+    first = jnp.where(wide < ROWS, 1.0, 0.0)
+    diagonal = lax.rem(wide, ROWS) == lax.broadcasted_iota(jnp.int32, (ROWS, 128), 0)
     cells = float(ROWS * N_DP * D)
 
     def cols(c):
@@ -121,15 +148,29 @@
             nsend.at[:, cols(c)], nrecv.at[j - 1, :, cols(c)], as_send.at[c, j - 1], as_recv.at[c, j - 1], at_small(j)
         )
 
-    def big_gather(c, j):
-        return remote(
-            g.at[0, :, cols(c)], g.at[j, :, cols(c)], ab_send.at[c, j - 1], ab_recv.at[c, j - 1], at_big(j)
-        )
-
-    def big_reduce(c, j):
-        return remote(
-            p.at[j, :, cols(c)], pr.at[j - 1, :, cols(c)], rb_send.at[c, j - 1], rb_recv.at[c, j - 1], at_big(-j)
-        )
+    def big_gather(c, i):
+        src, dst, at = (
+            (g.at[0, :, cols(c)], g.at[1, :, cols(c)], 1),
+            (g.at[0, :, cols(c)], g.at[3, :, cols(c)], -1),
+            (g.at[1, LOW, cols(c)], g.at[2, LOW, cols(c)], 1),
+            (g.at[3, HIGH, cols(c)], g.at[2, HIGH, cols(c)], -1),
+            (g.at[0, :, cols(c)], g.at[2, :, cols(c)], 2),
+        )[i]
+        return remote(src, dst, ab_send.at[c, i], ab_recv.at[c, i], at_big(at))
+
+    def big_reduce(c, i):
+        src, dst, at = (
+            (p.at[2, LOW, cols(c)], ph.at[0, :, cols(c)], 1),
+            (p.at[2, HIGH, cols(c)], ph.at[1, :, cols(c)], -1),
+            (p.at[3, HIGH, cols(c)], pr.at[0, HIGH, cols(c)], 1),
+            (p.at[1, LOW, cols(c)], pr.at[1, LOW, cols(c)], -1),
+            (p.at[3, LOW, cols(c)], pr.at[0, LOW, cols(c)], 1),
+            (p.at[1, HIGH, cols(c)], pr.at[1, HIGH, cols(c)], -1),
+            (p.at[2, :, cols(c)], pr.at[2, :, cols(c)], 2),
+            (p.at[3, :, cols(c)], pr.at[0, :, cols(c)], 1),
+            (p.at[1, :, cols(c)], pr.at[1, :, cols(c)], -1),
+        )[i]
+        return remote(src, dst, rb_send.at[c, i], rb_recv.at[c, i], at_big(at))
 
     def small_reduce(c, j):
         return remote(
@@ -145,73 +186,77 @@
                 osend.at[:, cols(c)], orecv.at[k, :, cols(c)], z_send.at[c], z_recv.at[k, c], after
             )
 
-        x = x_ref[...]
-        inverse = lax.rsqrt(jnp.mean(x * x, axis=-1, keepdims=True) + 1e-06)
-        for c in range(CHUNKS):
-            nsend[:, cols(c)] = (x_ref[:, cols(c)] * inverse * gain_ref[:, cols(c)]).astype(BF16)
+        def own_inverse():
+            x = x_ref[...]
+            return lax.rsqrt(jnp.mean(x * x, axis=-1, keepdims=True) + 1e-06)
+
+        def tell_inverse(slot):
+            i, j = lax.rem(slot, RING), lax.div(slot, RING)
+            at = lax.rem(small + i, RING) * step_small + lax.rem(big + j, RING) * step_big + core
+            return remote(inv_s.at[0], inv_s.at[slot], i_send, i_recv, (sec, at))
+
+        others = inv_s.at[pl.ds(1, RING * RING - 1)]
+
+        @pl.when(k == 0)
+        def _():
+            spread = jnp.sum(jnp.where(diagonal, own_inverse(), 0.0), axis=0, keepdims=True)
+            for slot in range(RING * RING):
+                inv_s[slot] = spread
 
         @pl.when(k > 0)
         def _():
-            for c in range(CHUNKS):
-                for j in (1, 3, 2):
-                    small_gather(c, j).start()
-            for c in range(CHUNKS):
-                for j in (1, 3, 2):
-                    small_gather(c, j).wait_recv()
-                rows = [nsend[:, cols(c)].astype(F32)] + [nrecv[j, :, cols(c)].astype(F32) for j in range(3)]
-                g[0, :, cols(c)] = jnp.concatenate(rows, axis=0).astype(BF16)
-                for j in (1, 3, 2):
-                    big_gather(c, j).start()
+            pltpu.make_async_copy(others, others, i_recv).wait()
+            pltpu.make_async_copy(others, others, i_send).wait()
+
+        for slot in range(RING * RING):
+            column = jnp.sum(jnp.where(diagonal, inv_s[slot], 0.0) * first, axis=1, keepdims=True)
+            inv_w[slot * ROWS : (slot + 1) * ROWS, :] = jnp.broadcast_to(column, (ROWS, 128))
+        inverse = inv_w[...]
+
+        def product_of(at):
+            value = coef[0, :1] * pre[0, :, at]
+            for l in range(1, HIST - 1):
+                value = value + coef[l, :1] * pre[l, :, at]
+            return value * inverse
+
+        for h in range(2):
+            for t in range(FFP // 128):
+                gate = product_of(pl.ds(2 * h * FFP + t * 128, 128))
+                up = product_of(pl.ds((2 * h + 1) * FFP + t * 128, 128))
+                value = gate / (1.0 + jnp.exp(-gate)) * up
+                real = lax.broadcasted_iota(jnp.int32, (TOK, 128), 1) < FFL - t * 128
+                hid[:, h * FFP + t * 128 : h * FFP + (t + 1) * 128] = jnp.where(real, value, 0.0).astype(BF16)
+
+        for c in range(CHUNKS):
+            @pl.when(k == 0)
+            def _():
+                local_copies[c].wait()
+                shared_copies[c].wait_recv()
+
+            product = jnp.dot(hid[...], wd[:, cols(c)], preferred_element_type=F32).astype(BF16)
+            p[:, :, cols(c)] = product.reshape(RING, PACK, CH)
+            for i in (0, 1, 2, 3) if c in RELAYED else (6, 7, 8):
+                big_reduce(c, i).start()
 
         @pl.when(k == 0)
         def _():
-            for c in range(CHUNKS):
-                mine = nsend[:, cols(c)].astype(F32)
-                packed = jnp.concatenate([mine] * RING, axis=0).astype(BF16)
-                for j in range(RING):
-                    g[j, :, cols(c)] = packed
-            for copy in local_copies:
+            for copy in local_copies[CHUNKS:]:
                 copy.wait()
-            for copy in shared_copies:
-                copy.wait_recv()
+            turn(0)
+
+        for c in RELAYED:
+            big_reduce(c, 0).wait_recv()
+            p[3, LOW, cols(c)] = (p[3, LOW, cols(c)].astype(F32) + ph[0, :, cols(c)].astype(F32)).astype(BF16)
+            big_reduce(c, 4).start()
+            big_reduce(c, 1).wait_recv()
+            p[1, HIGH, cols(c)] = (p[1, HIGH, cols(c)].astype(F32) + ph[1, :, cols(c)].astype(F32)).astype(BF16)
+            big_reduce(c, 5).start()
 
         for c in range(CHUNKS):
-            @pl.when(k > 0)
-            def _():
-                for j in (1, 3, 2):
-                    big_gather(c, j).wait_recv()
-
-            tokens = g[:, :, cols(c)].reshape(TOK, CH)
-
-            @pl.loop(0, 4 * FFP // NT)
-            def _(n):
-                at = pl.ds(pl.multiple_of(n * NT, NT), NT)
-                product = lax.dot_general(
-                    tokens, wgu[at, cols(c)], (((1,), (1,)), ((), ())), preferred_element_type=F32
-                )
-                if c == 0:
-                    acc[:, at] = product
-                else:
-                    acc[:, at] += product
-
-        for h in range(2):
-            gate = acc[:, h * FFP : (h + 1) * FFP]
-            up = acc[:, (2 + h) * FFP : (3 + h) * FFP]
-            value = gate / (1.0 + jnp.exp(-gate)) * up
-            real = lax.broadcasted_iota(jnp.int32, (TOK, FFP), 1) < FFL
-            hid[:, h * FFP : (h + 1) * FFP] = jnp.where(real, value, 0.0).astype(BF16)
-
-        for c in range(CHUNKS):
-            product = jnp.dot(hid[...], wd[:, cols(c)], preferred_element_type=F32).astype(BF16)
-            p[:, :, cols(c)] = product.reshape(RING, PACK, CH)
-            for j in (1, 3, 2):
-                big_reduce(c, j).start()
-
-        for c in range(CHUNKS):
-            for j in (1, 3, 2):
-                big_reduce(c, j).wait_recv()
+            for i in (2, 3, 4, 5) if c in RELAYED else (6, 7, 8):
+                big_reduce(c, i).wait_recv()
             total = p[0, :, cols(c)].astype(F32)
-            for j in range(3):
+            for j in range(2 if c in RELAYED else 3):
                 total = total + pr[j, :, cols(c)].astype(F32)
             qown[:, cols(c)] = total[:ROWS]
             for j in (1, 3, 2):
@@ -234,6 +279,14 @@
             misfit = mapped - x_ref[:, cols(c)]
             images[k, :, cols(c)] = mapped
             misfits[k, :, cols(c)] = misfit
+            nsend[:, cols(c)] = ((mapped - prev[:, cols(c)]) * gain_ref[:, cols(c)]).astype(BF16)
+            prev[:, cols(c)] = mapped
+
+            @pl.when(k < ITERS - 1)
+            def _():
+                for j in (1, 3, 2):
+                    small_gather(c, j).start()
+
             sums = [sums[i] + misfit * misfits[i, :, cols(c)] for i in range(HIST)]
         row = jnp.zeros((1, 128), F32)
         for i in range(HIST):
@@ -247,17 +300,35 @@
                 gmsg, grecv.at[parity, d - 1], g_send, g_recv.at[parity], (sec, lax.rem(dp + d, N_DP))
             ).start()
 
-        @pl.when(k > 0)
+        for c in range(CHUNKS):
+            for i in range(6) if c in RELAYED else (6, 7, 8):
+                big_reduce(c, i).wait_send()
+            for j in (1, 3, 2):
+                small_reduce(c, j).wait_send()
+            relay(c).wait_send()
+
+        @pl.when(k < ITERS - 1)
         def _():
+            @pl.when(k == 0)
+            def _():
+                for copy in shared_copies[CHUNKS:]:
+                    copy.wait_recv()
+                turn(1)
+
             for c in range(CHUNKS):
                 for j in (1, 3, 2):
-                    small_gather(c, j).wait_send()
-                    big_gather(c, j).wait_send()
-        for c in range(CHUNKS):
-            for j in (1, 3, 2):
-                big_reduce(c, j).wait_send()
-                small_reduce(c, j).wait_send()
-            relay(c).wait_send()
+                    small_gather(c, j).wait_recv()
+                rows = [nsend[:, cols(c)].astype(F32)] + [nrecv[j, :, cols(c)].astype(F32) for j in range(3)]
+                g[0, :, cols(c)] = jnp.concatenate(rows, axis=0).astype(BF16)
+                for i in (0, 1) if c in RELAYED else (4, 0, 1):
+                    big_gather(c, i).start()
+
+            for c in RELAYED:
+                big_gather(c, 0).wait_recv()
+                big_gather(c, 2).start()
+                big_gather(c, 1).wait_recv()
+                big_gather(c, 3).start()
+
         pltpu.make_async_copy(grecv.at[parity], grecv.at[parity], g_recv.at[parity]).wait()
         row = (row + jnp.sum(grecv[parity], axis=0)) / cells
         pltpu.make_async_copy(grecv.at[parity], grecv.at[parity], g_send).wait()
@@ -292,12 +363,45 @@
         for i in range(HIST):
             mixed = jnp.where(lane == i, weights[i][:1], mixed)
         mixing_ref[pl.ds(k, 1), :] = mixed[:, :HIST]
+        for l in range(HIST - 1):
+            tail = weights[l]
+            for i in range(l + 1, HIST):
+                tail = tail + weights[i]
+            coef[l] = tail
         for c in range(D // 128):
             at = pl.ds(c * 128, 128)
             value = weights[0] * images[0, :, at]
             for i in range(1, HIST):
                 value = value + weights[i] * images[i, :, at]
             x_ref[:, at] = value
+
+        @pl.when(k < ITERS - 1)
+        def _():
+            inv_s[0] = jnp.sum(jnp.where(diagonal, own_inverse(), 0.0), axis=0, keepdims=True)
+
+            @pl.loop(1, RING * RING)
+            def _(slot):
+                tell_inverse(slot).start()
+
+            for c in range(CHUNKS):
+                for i in (2, 3) if c in RELAYED else (0, 1, 4):
+                    big_gather(c, i).wait_recv()
+                tokens = g[:, :, cols(c)].reshape(TOK, CH)
+
+                @pl.loop(0, 4 * FFP // NT)
+                def _(n):
+                    at = pl.ds(pl.multiple_of(n * NT, NT), NT)
+                    product = jnp.dot(tokens, wgt[cols(c), at], preferred_element_type=F32)
+                    if c == 0:
+                        pre[k, :, at] = product
+                    else:
+                        pre[k, :, at] += product
+
+            for c in range(CHUNKS):
+                for j in (1, 3, 2):
+                    small_gather(c, j).wait_send()
+                for i in range(4) if c in RELAYED else (0, 1, 4):
+                    big_gather(c, i).wait_send()
 
     for copy in shared_copies:
         copy.wait_send()
@@ -315,16 +419,20 @@
         out_specs=(vmem, vmem),
         scratch_shapes=[
             pltpu.VMEM((4 * FFP, D), BF16),
+            pltpu.VMEM((D, 4 * FFP), BF16),
+            pltpu.VMEM((256, 256), BF16),
             pltpu.VMEM((2 * FFP, D), BF16),
-            pltpu.VMEM((TOK, 4 * FFP), F32),
+            pltpu.VMEM((HIST - 1, TOK, 4 * FFP), F32),
             pltpu.VMEM((TOK, 2 * FFP), BF16),
             pltpu.VMEM((HIST, ROWS, D), F32),
             pltpu.VMEM((HIST, ROWS, D), F32),
+            pltpu.VMEM((ROWS, D), F32),
             pltpu.VMEM((ROWS, D), F32),
             pltpu.VMEM((ROWS, D), BF16),
             pltpu.VMEM((3, ROWS, D), BF16),
             pltpu.VMEM((RING, PACK, D), BF16),
             pltpu.VMEM((RING, PACK, D), BF16),
+            pltpu.VMEM((2, HALF, D), BF16),
             pltpu.VMEM((3, PACK, D), BF16),
             pltpu.VMEM((3, ROWS, D), BF16),
             pltpu.VMEM((ROWS, D), F32),
@@ -334,10 +442,13 @@
             pltpu.VMEM((1, 128), F32),
             pltpu.VMEM((2, N_DP - 1, 1, 128), F32),
             pltpu.VMEM((HIST * (HIST + 1) // 2, 8, 128), F32),
-            dma((3,)), dma((3,)), dma((3,)),
-            dma((CHUNKS, 3)), dma((CHUNKS, 3)), dma((CHUNKS, 3)), dma((CHUNKS, 3)),
-            dma((CHUNKS, 3)), dma((CHUNKS, 3)), dma((CHUNKS, 3)), dma((CHUNKS, 3)),
-            dma((CHUNKS,)), dma((ITERS, CHUNKS)), dma, dma((2,)),
+            pltpu.VMEM((HIST - 1, 8, 128), F32),
+            pltpu.VMEM((RING * RING, 1, 128), F32),
+            pltpu.VMEM((TOK, 128), F32),
+            dma((2 + CHUNKS,)), dma((2 + CHUNKS,)), dma((2 + CHUNKS,)),
+            dma((CHUNKS, 3)), dma((CHUNKS, 3)), dma((CHUNKS, 5)), dma((CHUNKS, 5)),
+            dma((CHUNKS, 9)), dma((CHUNKS, 9)), dma((CHUNKS, 3)), dma((CHUNKS, 3)),
+            dma((CHUNKS,)), dma((ITERS, CHUNKS)), dma, dma((2,)), dma, dma,
         ],
         compiler_params=pltpu.CompilerParams(
             collective_id=0, has_side_effects=True, vmem_limit_bytes=62 * 1024 * 1024

time: 204 us -> 159 us (0.78)
  Pallas kernels: 201 us -> 155 us
    pallas_call x1, Pallas kernels: 201 us -> 155 us  [local(): pl.pallas_call(kernel, out_shape=(jax.ShapeDtypeStruct((ROWS, D), F32), j...]
where the time goes in v2:
time: 159 us
  Pallas kernels  155 us (97%)
  local copies, waits for them, and re-layouts  2.83 us (2%)
    pallas_call x1, Pallas kernels, local(): pl.pallas_call(kernel, out_shape=(jax.ShapeDtypeStruct((ROWS, D), F32), j...  155 us

profile of v2, /device:TPU:1, one launch (start us, length us, event | category | flops | bytes accessed | tf_op | source)
XLA Modules:
  0.0 158.5 jit_solution(3943095753739531188)
XLA Ops:
  0.6 155.0 %shard_map.68 = (f32[8,4096]{1,0:T(8,128)}, f32[5,5]{1,0:T(8,128)}) custom-call(bf16[8,4096]{1,0:T(8,128)(2,1)} %bitcast.14, f32[1,4096]{1,0:T(1,128)} %gain_ref.1, bf16[344,4096]{1,0:T(8,128)(2,1)} %bitcast.10, bf16[344,4096]{1,0:T(8,128)(2,1)} %bitcast.11, bf16[344,4096]{1,0:T(8,128)(2,1)} %bitcast.12), custom_call_target="tpu_custom_call" | custom-call | tf_op jit(solution)/shard_map/pallas_call | solution.py:415
  155.7 1.3 copy.7
  156.9 1.6 copy.9

commit v3 on v1

v3 whole, which is shorter than its diff:
```python
import jax
import jax.numpy as jnp
from jax import lax
from jax.experimental import pallas as pl
from jax.experimental.pallas import tpu as pltpu
from jax.sharding import PartitionSpec as P

ITERS = 5
HIST = 5
STEPS = ITERS - 1
SECTIONS = 8
RING = 4
N_DP = 32
ROWS = 8
PACK = RING * ROWS
TOK = RING * PACK
D = 4096
FFL = 344
FFP = 384
WIDTHS = (1024, 1024, 1024, 1024)
CHUNKS = len(WIDTHS)
STARTS = tuple(sum(WIDTHS[:c]) for c in range(CHUNKS))
NT = 512
LATER = 7.4
MESH = pl.DeviceIdType.MESH
F32 = jnp.float32
BF16 = jnp.bfloat16


def solve_small(entries, values):
    count = len(values)
    entries = [list(row) for row in entries]
    values = list(values)
    for p in range(count):
        for i in range(p + 1, count):
            factor = entries[i][p] / entries[p][p]
            for j in range(p, count):
                entries[i][j] = entries[i][j] - factor * entries[p][j]
            values[i] = values[i] - factor * values[p]
    answer = [None] * count
    for i in range(count - 1, -1, -1):
        accum = values[i]
        for j in range(i + 1, count):
            accum = accum - entries[i][j] * answer[j]
        answer[i] = accum / entries[i][i]
    return answer


def folded(value):
    total = value[:, :128]
    for t in range(1, value.shape[1] // 128):
        total = total + value[:, t * 128 : (t + 1) * 128]
    return total


def order_of_work():
    work = []
    for c in range(CHUNKS):
        at = 7.0 * (STARTS[c] + WIDTHS[c]) / D
        work += [(at, 0, c), (at + 3.9, 1, c), (at + LATER, 2, c)]
    return [(stage, c) for _, stage, c in sorted(work)]


def kernel(
    inject_ref, gain_ref, wg_hbm, wu_hbm, wd_hbm,
    iterate_ref, mixing_ref,
    wgu, wgt, eye, wd, pre, hid, images, misfits, x_ref, inj, prev, past,
    g, p, pr, q, qown, qr, osend, orecv, gsum, gmsg, grecv, gram_s, coef, cross, wts, msum, mh,
    w_local, w_send, w_recv, n_send, n_recv,
    ab_send, ab_recv, rb_send, rb_recv, rs_send, rs_recv,
    z_send, z_recv, g_send, g_recv, m_send, m_recv,
):
    sec = lax.axis_index("section")
    dp = lax.axis_index("dp")
    core = lax.rem(dp, 2)
    cx = lax.div(dp, 8)
    cy = lax.rem(lax.div(dp, 2), RING)
    small = cx + core * (cy - cx)
    big = cy + core * (cx - cy)
    step_small = 8 - 6 * core
    step_big = 2 + 6 * core
    next_sec = lax.rem(sec + 1, SECTIONS)
    last_sec = lax.rem(sec + SECTIONS - 1, SECTIONS)

    def in_small(j):
        return lax.rem(small + RING + j, RING) * step_small + big * step_big + core

    def at_big(j):
        return (sec, small * step_small + lax.rem(big + RING + j, RING) * step_big + core)

    sibling = (sec, dp + 1 - 2 * core)

    def remote(src, dst, send, recv, device):
        return pltpu.make_async_remote_copy(
            src_ref=src, dst_ref=dst, send_sem=send, recv_sem=recv, device_id=device, device_id_type=MESH
        )

    def cols(c):
        return pl.ds(STARTS[c], WIDTHS[c])

    local_copies = []
    shared_copies = []
    for c in range(CHUNKS):
        local_copies.append(
            pltpu.make_async_copy(wd_hbm.at[:, cols(c)], wd.at[pl.ds(0, FFL), cols(c)], w_local.at[2 + c])
        )
        shared_copies.append(
            remote(
                wd_hbm.at[:, cols(c)], wd.at[pl.ds(FFP, FFL), cols(c)], w_send.at[2 + c], w_recv.at[2 + c], sibling
            )
        )
    for i, ref in ((0, wg_hbm), (1, wu_hbm)):
        local_copies.append(pltpu.make_async_copy(ref, wgu.at[pl.ds(i * FFP, FFL), :], w_local.at[i]))
        shared_copies.append(
            remote(ref, wgu.at[pl.ds((2 + i) * FFP, FFL), :], w_send.at[i], w_recv.at[i], sibling)
        )
    for copy in local_copies:
        copy.start()

    barrier = pltpu.get_barrier_semaphore()

    def greet(device):
        pl.semaphore_signal(barrier, inc=1, device_id=device, device_id_type=MESH)

    @pl.loop(1, N_DP)
    def _(d):
        greet((sec, lax.rem(dp + d, N_DP)))

    for i in range(RING):
        greet((next_sec, in_small(i)))
        greet((last_sec, in_small(-i)))

    for ref in (x_ref, prev, images, misfits, past, gram_s, coef, cross, wts, mh, pre):
        ref[...] = jnp.zeros_like(ref)
    for h in range(2):
        wgu[2 * h * FFP + FFL : (2 * h + 1) * FFP, :] = jnp.zeros((FFP - FFL, D), BF16)
        wgu[(2 * h + 1) * FFP + FFL : (2 * h + 2) * FFP, :] = jnp.zeros((FFP - FFL, D), BF16)
        wd[h * FFP + FFL : (h + 1) * FFP, :] = jnp.zeros((FFP - FFL, D), BF16)
    corner = lax.broadcasted_iota(jnp.int32, (256, 256), 0) == lax.broadcasted_iota(jnp.int32, (256, 256), 1)
    eye[...] = jnp.where(corner, 1.0, 0.0).astype(BF16)
    inj[0] = inject_ref[...]

    def turn(half, start, stop):
        @pl.loop(start, stop)
        def _(n):
            at = pl.ds(pl.multiple_of(n * 256, 256), 256)
            rows = pl.ds(half * 2 * FFP, 2 * FFP)
            wgt[at, rows] = lax.dot_general(
                eye[...], wgu[rows, at], (((1,), (1,)), ((), ())), preferred_element_type=F32
            ).astype(BF16)

    def share_inject(i):
        return remote(inject_ref, inj.at[i], n_send.at[i - 1], n_recv.at[i - 1], (sec, in_small(i)))

    pl.semaphore_wait(barrier, N_DP - 1 + 2 * RING)
    for copy in shared_copies:
        copy.start()
    for i in range(1, RING):
        share_inject(i).start()

    lane = lax.broadcasted_iota(jnp.int32, (1, 128), 1)
    cells = float(ROWS * N_DP * D)

    def big_gather(c, j):
        return remote(
            g.at[0, :, cols(c)], g.at[j, :, cols(c)], ab_send.at[c, j - 1], ab_recv.at[c, j - 1], at_big(j)
        )

    def big_reduce(c, j):
        return remote(
            p.at[j, :, cols(c)], pr.at[j - 1, :, cols(c)], rb_send.at[c, j - 1], rb_recv.at[c, j - 1], at_big(-j)
        )

    def small_reduce(c, j):
        return remote(
            q.at[j - 1, :, cols(c)], qr.at[j - 1, :, cols(c)], rs_send.at[c, j - 1], rs_recv.at[c, j - 1],
            (sec, in_small(-j)),
        )

    def combine(at):
        value = wts[0] * images[0, :, at]
        for i in range(1, HIST):
            value = value + wts[i] * images[i, :, at]
        return value

    @pl.loop(0, ITERS)
    def _(k):
        parity = lax.rem(k, 2)
        going = k < STEPS

        def hand_on(c, i):
            return remote(
                osend.at[:, cols(c)], orecv.at[k, i, :, cols(c)], z_send.at[c, i], z_recv.at[k, c],
                (next_sec, in_small(i)),
            )

        def tell_norms(j):
            return remote(mh.at[k, 0], mh.at[k, j], m_send, m_recv, at_big(j))

        @pl.when(k > 0)
        def _():
            others = mh.at[k - 1, pl.ds(1, RING - 1)]
            pltpu.make_async_copy(others, others, m_recv).wait()
            pltpu.make_async_copy(others, others, m_send).wait()

        square = mh[0].reshape(TOK, 128) * cross[0]
        for l in range(1, STEPS):
            square = square + mh[l].reshape(TOK, 128) * cross[l]
        square = jnp.maximum(jnp.sum(square, axis=1, keepdims=True), 0.0)
        inverse = jnp.broadcast_to(lax.rsqrt(square / float(D) + 1e-06), (TOK, 128))

        def product_of(at):
            value = coef[0, :1] * pre[0, :, at]
            for l in range(1, STEPS):
                value = value + coef[l, :1] * pre[l, :, at]
            return value * inverse

        for h in range(2):
            for t in range(FFP // 128):
                gate = product_of(pl.ds(2 * h * FFP + t * 128, 128))
                up = product_of(pl.ds((2 * h + 1) * FFP + t * 128, 128))
                value = gate / (1.0 + jnp.exp(-gate)) * up
                real = lax.broadcasted_iota(jnp.int32, (TOK, 128), 1) < FFL - t * 128
                hid[:, h * FFP + t * 128 : h * FFP + (t + 1) * 128] = jnp.where(real, value, 0.0).astype(BF16)

        for c in range(CHUNKS):
            @pl.when(k == 0)
            def _():
                local_copies[c].wait()
                shared_copies[c].wait_recv()

            product = jnp.dot(hid[...], wd[:, cols(c)], preferred_element_type=F32).astype(BF16)
            p[:, :, cols(c)] = product.reshape(RING, PACK, WIDTHS[c])
            for j in (2, 1, 3):
                big_reduce(c, j).start()

        @pl.when(k == 0)
        def _():
            for copy in local_copies[CHUNKS:]:
                copy.wait()
            turn(0, 0, 8)

        for c in range(D // 128):
            at = pl.ds(c * 128, 128)
            x_ref[:, at] = combine(at)
        gsum[...] = jnp.zeros_like(gsum)
        msum[...] = jnp.zeros_like(msum)

        def sum_big(c):
            for j in (1, 3, 2):
                big_reduce(c, j).wait_recv()
            total = p[0, :, cols(c)].astype(F32)
            for j in range(3):
                total = total + pr[j, :, cols(c)].astype(F32)
            qown[:, cols(c)] = total[:ROWS]
            for j in (2, 1, 3):
                q[j - 1, :, cols(c)] = total[j * ROWS : (j + 1) * ROWS].astype(BF16)
                small_reduce(c, j).start()

            if c in (0, 1):
                @pl.when(k == 0)
                def _():
                    turn(0, 8 + 4 * c, 12 + 4 * c)

        def sum_small(c):
            for j in (1, 3, 2):
                small_reduce(c, j).wait_recv()
            total = qown[:, cols(c)]
            for j in range(3):
                total = total + qr[j, :, cols(c)].astype(F32)
            osend[:, cols(c)] = (x_ref[:, cols(c)] + total).astype(BF16)

            @pl.when(going)
            def _():
                for i in (2, 1, 3):
                    hand_on(c, i).start()

            hand_on(c, 0).start()
            if c == 0:
                @pl.when(k == 0)
                def _():
                    for i in range(1, RING):
                        share_inject(i).wait_recv()
                    for copy in shared_copies[CHUNKS:]:
                        copy.wait_recv()

            if c < 4:
                @pl.when(k == 0)
                def _():
                    turn(1, 4 * c, 4 * c + 4)

        def gather(c):
            @pl.when(going)
            def _():
                came = orecv.at[k, :, :, cols(c)]
                pltpu.make_async_copy(came, came, z_recv.at[k, c]).wait()

            @pl.when(k == STEPS)
            def _():
                came = orecv.at[k, 0, :, cols(c)]
                pltpu.make_async_copy(came, came, z_recv.at[k, c]).wait()

            @pl.when(going)
            def _():
                rows = []
                for i in range(RING):
                    at = pl.ds(i * ROWS, ROWS)
                    mapped = inj[i, :, cols(c)].astype(F32) + 0.5 * orecv[k, i, :, cols(c)].astype(F32)
                    step = mapped - prev[at, cols(c)]
                    prev[at, cols(c)] = mapped
                    past[k, at, cols(c)] = step
                    rows.append(step * gain_ref[:, cols(c)])
                g[0, :, cols(c)] = jnp.concatenate(rows, axis=0).astype(BF16)
                for j in (2, 1, 3):
                    big_gather(c, j).start()
                for i in range(RING):
                    at = pl.ds(i * ROWS, ROWS)
                    step = past[k, at, cols(c)]
                    for l in range(STEPS):
                        msum[l, at, :] += folded(step * past[l, at, cols(c)])

            mapped = inj[0, :, cols(c)].astype(F32) + 0.5 * orecv[k, 0, :, cols(c)].astype(F32)
            misfit = mapped - x_ref[:, cols(c)]
            images[k, :, cols(c)] = mapped
            misfits[k, :, cols(c)] = misfit
            for i in range(HIST):
                gsum[i] += folded(misfit * misfits[i, :, cols(c)])

        for stage, c in order_of_work():
            (sum_big, sum_small, gather)[stage](c)

        row = jnp.zeros((1, 128), F32)
        for i in range(HIST):
            value = jnp.sum(jnp.sum(gsum[i], axis=0, keepdims=True), axis=1, keepdims=True)
            row = jnp.where(lane == i, value, row)
        gmsg[...] = row

        @pl.loop(1, N_DP)
        def _(d):
            remote(
                gmsg, grecv.at[parity, d - 1], g_send, g_recv.at[parity], (sec, lax.rem(dp + d, N_DP))
            ).start()

        @pl.when(going)
        def _():
            table = jnp.zeros((PACK, 128), F32)
            for l in range(STEPS):
                table = jnp.where(lane == l, jnp.sum(msum[l], axis=1, keepdims=True), table)
            mh[k, 0] = table
            for j in (2, 1, 3):
                tell_norms(j).start()

        for c in range(CHUNKS):
            for j in (1, 3, 2):
                big_reduce(c, j).wait_send()
                small_reduce(c, j).wait_send()
            hand_on(c, 0).wait_send()

        @pl.when(going)
        def _():
            for c in range(CHUNKS):
                for j in (1, 3, 2):
                    big_gather(c, j).wait_recv()
                tokens = g[:, :, cols(c)].reshape(TOK, WIDTHS[c])

                @pl.loop(0, 4 * FFP // NT)
                def _(n):
                    at = pl.ds(pl.multiple_of(n * NT, NT), NT)
                    product = jnp.dot(tokens, wgt[cols(c), at], preferred_element_type=F32)
                    if c == 0:
                        pre[k, :, at] = product
                    else:
                        pre[k, :, at] += product

            for c in range(CHUNKS):
                for j in (1, 3, 2):
                    big_gather(c, j).wait_send()
                    hand_on(c, j).wait_send()

        pltpu.make_async_copy(grecv.at[parity], grecv.at[parity], g_recv.at[parity]).wait()
        row = (row + jnp.sum(grecv[parity], axis=0)) / cells
        pltpu.make_async_copy(grecv.at[parity], grecv.at[parity], g_send).wait()

        fresh = [
            jnp.broadcast_to(jnp.sum(jnp.where(lane == i, row, 0.0), axis=1, keepdims=True), (8, 128))
            for i in range(HIST)
        ]
        gram = [[None] * HIST for _ in range(HIST)]
        for i in range(HIST):
            for j in range(i + 1):
                slot = i * (i + 1) // 2 + j
                entry = jnp.where(k == i, fresh[j], gram_s[slot])
                gram_s[slot] = entry
                gram[i][j] = entry
                gram[j][i] = entry
        steps = jnp.full((8, 128), k + 1, jnp.int32)
        live = [jnp.where(steps > i, 1.0, 0.0) for i in range(HIST)]
        trace = gram[0][0]
        for i in range(1, HIST):
            trace = trace + gram[i][i]
        damp = 0.01 * trace / steps.astype(F32) + 1e-06
        system = [[gram[i][j] * live[i] * live[j] for j in range(HIST)] for i in range(HIST)]
        for i in range(HIST):
            system[i][i] = system[i][i] + (live[i] * damp + (1.0 - live[i]))
        beta = solve_small(system, live)
        whole = beta[0]
        for i in range(1, HIST):
            whole = whole + beta[i]
        weights = [value / whole for value in beta]
        mixed = jnp.zeros((1, 128), F32)
        for i in range(HIST):
            wts[i] = weights[i]
            mixed = jnp.where(lane == i, weights[i][:1], mixed)
        mixing_ref[pl.ds(k, 1), :] = mixed[:, :HIST]
        tails = [weights[HIST - 1]]
        for i in range(HIST - 2, -1, -1):
            tails.insert(0, tails[0] + weights[i])
        for l in range(STEPS):
            coef[l] = tails[l]
            line = jnp.zeros((1, 128), F32)
            for i in range(l + 1):
                line = jnp.where(lane == i, (1.0 if i == l else 2.0) * tails[l][:1] * tails[i][:1], line)
            cross[l] = line

    for copy in shared_copies:
        copy.wait_send()
    for i in range(1, RING):
        share_inject(i).wait_send()
    for c in range(D // 128):
        at = pl.ds(c * 128, 128)
        iterate_ref[:, at] = combine(at)


def local(inject, w_gate, w_up, w_down, gain):
    vmem = pl.BlockSpec(memory_space=pltpu.VMEM)
    hbm = pl.BlockSpec(memory_space=pl.ANY)
    dma = pltpu.SemaphoreType.DMA
    iterate, mixing = pl.pallas_call(
        kernel,
        out_shape=(jax.ShapeDtypeStruct((ROWS, D), F32), jax.ShapeDtypeStruct((ITERS, HIST), F32)),
        in_specs=[vmem, vmem, hbm, hbm, hbm],
        out_specs=(vmem, vmem),
        scratch_shapes=[
            pltpu.VMEM((4 * FFP, D), BF16),
            pltpu.VMEM((D, 4 * FFP), BF16),
            pltpu.VMEM((256, 256), BF16),
            pltpu.VMEM((2 * FFP, D), BF16),
            pltpu.VMEM((STEPS, TOK, 4 * FFP), F32),
            pltpu.VMEM((TOK, 2 * FFP), BF16),
            pltpu.VMEM((HIST, ROWS, D), F32),
            pltpu.VMEM((HIST, ROWS, D), F32),
            pltpu.VMEM((ROWS, D), F32),
            pltpu.VMEM((RING, ROWS, D), BF16),
            pltpu.VMEM((PACK, D), F32),
            pltpu.VMEM((STEPS, PACK, D), F32),
            pltpu.VMEM((RING, PACK, D), BF16),
            pltpu.VMEM((RING, PACK, D), BF16),
            pltpu.VMEM((3, PACK, D), BF16),
            pltpu.VMEM((3, ROWS, D), BF16),
            pltpu.VMEM((ROWS, D), F32),
            pltpu.VMEM((3, ROWS, D), BF16),
            pltpu.VMEM((ROWS, D), BF16),
            pltpu.VMEM((ITERS, RING, ROWS, D), BF16),
            pltpu.VMEM((HIST, ROWS, 128), F32),
            pltpu.VMEM((1, 128), F32),
            pltpu.VMEM((2, N_DP - 1, 1, 128), F32),
            pltpu.VMEM((HIST * (HIST + 1) // 2, 8, 128), F32),
            pltpu.VMEM((STEPS, 8, 128), F32),
            pltpu.VMEM((STEPS, 1, 128), F32),
            pltpu.VMEM((HIST, 8, 128), F32),
            pltpu.VMEM((STEPS, PACK, 128), F32),
            pltpu.VMEM((STEPS, RING, PACK, 128), F32),
            dma((2 + CHUNKS,)), dma((2 + CHUNKS,)), dma((2 + CHUNKS,)), dma((3,)), dma((3,)),
            dma((CHUNKS, 3)), dma((CHUNKS, 3)), dma((CHUNKS, 3)), dma((CHUNKS, 3)), dma((CHUNKS, 3)), dma((CHUNKS, 3)),
            dma((CHUNKS, RING)), dma((ITERS, CHUNKS)), dma, dma((2,)), dma, dma,
        ],
        compiler_params=pltpu.CompilerParams(
            collective_id=0, has_side_effects=True, vmem_limit_bytes=62 * 1024 * 1024
        ),
    )(inject[0], gain, w_gate[0].T, w_up[0].T, w_down[0])
    return iterate[None], mixing[None]


def solution(mesh):
    return jax.shard_map(
        local,
        mesh=mesh,
        in_specs=(
            P("section", "dp", None),
            P("section", None, "dp"),
            P("section", None, "dp"),
            P("section", "dp", None),
            P("section", None),
        ),
        out_specs=(P("section", "dp", None), P("section", None, None)),
        check_vma=False,
    )
```

time: 204 us -> 143 us (0.70)
  Pallas kernels: 201 us -> 139 us
    pallas_call x1, Pallas kernels: 201 us -> 139 us  [local(): pl.pallas_call(kernel, out_shape=(jax.ShapeDtypeStruct((ROWS, D), F32), j...]
where the time goes in v3:
time: 143 us
  Pallas kernels  139 us (97%)
  local copies, waits for them, and re-layouts  2.83 us (2%)
    pallas_call x1, Pallas kernels, local(): pl.pallas_call(kernel, out_shape=(jax.ShapeDtypeStruct((ROWS, D), F32), j...  139 us

profile of v3, /device:TPU:1, one launch (start us, length us, event | category | flops | bytes accessed | tf_op | source)
XLA Modules:
  0.0 142.8 jit_solution(734729712513007612)
XLA Ops:
  0.6 139.3 %shard_map.68 = (f32[8,4096]{1,0:T(8,128)}, f32[5,5]{1,0:T(8,128)}) custom-call(bf16[8,4096]{1,0:T(8,128)(2,1)} %bitcast.14, f32[1,4096]{1,0:T(1,128)} %gain_ref.1, bf16[344,4096]{1,0:T(8,128)(2,1)} %bitcast.10, bf16[344,4096]{1,0:T(8,128)(2,1)} %bitcast.11, bf16[344,4096]{1,0:T(8,128)(2,1)} %bitcast.12), custom_call_target="tpu_custom_call" | custom-call | tf_op jit(solution)/shard_map/pallas_call | solution.py:438
  139.9 1.3 copy.7
  141.2 1.6 %copy.9 = f32[1,8,4096]{2,1,0:T(8,128)} copy(f32[1,8,4096]{2,1,0:T(8,128)} %bitcast.13) | data formatting | bytes 262144

commit v4 on v3

--- a/solution.py
+++ b/solution.py
@@ -17,11 +17,12 @@
 D = 4096
 FFL = 344
 FFP = 384
-WIDTHS = (1024, 1024, 1024, 1024)
+WIDTHS = (1024, 1024, 1024, 512, 512)
 CHUNKS = len(WIDTHS)
 STARTS = tuple(sum(WIDTHS[:c]) for c in range(CHUNKS))
-NT = 512
+NT = 1536
 LATER = 7.4
+FAR_FIRST = [(i, j, l) for i in (2, 1, 3, 0) for j in (2, 1, 3, 0) for l in (1, 0)][:-1]
 MESH = pl.DeviceIdType.MESH
 F32 = jnp.float32
 BF16 = jnp.bfloat16
@@ -57,7 +58,7 @@
     work = []
     for c in range(CHUNKS):
         at = 7.0 * (STARTS[c] + WIDTHS[c]) / D
-        work += [(at, 0, c), (at + 3.9, 1, c), (at + LATER, 2, c)]
+        work += [(at, 0, c), (at + 3.9, 1, c), (at + LATER, 2, c), (at + 12.0, 3, c)]
     return [(stage, c) for _, stage, c in sorted(work)]
 
 
@@ -326,39 +327,9 @@
             for i in range(HIST):
                 gsum[i] += folded(misfit * misfits[i, :, cols(c)])
 
-        for stage, c in order_of_work():
-            (sum_big, sum_small, gather)[stage](c)
-
-        row = jnp.zeros((1, 128), F32)
-        for i in range(HIST):
-            value = jnp.sum(jnp.sum(gsum[i], axis=0, keepdims=True), axis=1, keepdims=True)
-            row = jnp.where(lane == i, value, row)
-        gmsg[...] = row
-
-        @pl.loop(1, N_DP)
-        def _(d):
-            remote(
-                gmsg, grecv.at[parity, d - 1], g_send, g_recv.at[parity], (sec, lax.rem(dp + d, N_DP))
-            ).start()
-
-        @pl.when(going)
-        def _():
-            table = jnp.zeros((PACK, 128), F32)
-            for l in range(STEPS):
-                table = jnp.where(lane == l, jnp.sum(msum[l], axis=1, keepdims=True), table)
-            mh[k, 0] = table
-            for j in (2, 1, 3):
-                tell_norms(j).start()
-
-        for c in range(CHUNKS):
-            for j in (1, 3, 2):
-                big_reduce(c, j).wait_send()
-                small_reduce(c, j).wait_send()
-            hand_on(c, 0).wait_send()
-
-        @pl.when(going)
-        def _():
-            for c in range(CHUNKS):
+        def multiply(c):
+            @pl.when(going)
+            def _():
                 for j in (1, 3, 2):
                     big_gather(c, j).wait_recv()
                 tokens = g[:, :, cols(c)].reshape(TOK, WIDTHS[c])
@@ -372,13 +343,48 @@
                     else:
                         pre[k, :, at] += product
 
+        def tell():
+            row = jnp.zeros((1, 128), F32)
+            for i in range(HIST):
+                value = jnp.sum(jnp.sum(gsum[i], axis=0, keepdims=True), axis=1, keepdims=True)
+                row = jnp.where(lane == i, value, row)
+            gmsg[...] = row
+
+            for n, (i, j, l) in enumerate(FAR_FIRST):
+                x, y, other = lax.rem(cx + i, RING), lax.rem(cy + j, RING), lax.rem(core + l, 2)
+                remote(
+                    gmsg, grecv.at[parity, n], g_send, g_recv.at[parity], (sec, x * 8 + y * 2 + other)
+                ).start()
+
+            @pl.when(going)
+            def _():
+                table = jnp.zeros((PACK, 128), F32)
+                for l in range(STEPS):
+                    table = jnp.where(lane == l, jnp.sum(msum[l], axis=1, keepdims=True), table)
+                mh[k, 0] = table
+                for j in (2, 1, 3):
+                    tell_norms(j).start()
+
+        for stage, c in order_of_work():
+            (sum_big, sum_small, gather, multiply)[stage](c)
+            if stage == 2 and c == CHUNKS - 1:
+                tell()
+
+        for c in range(CHUNKS):
+            for j in (1, 3, 2):
+                big_reduce(c, j).wait_send()
+                small_reduce(c, j).wait_send()
+            hand_on(c, 0).wait_send()
+
+        @pl.when(going)
+        def _():
             for c in range(CHUNKS):
                 for j in (1, 3, 2):
                     big_gather(c, j).wait_send()
                     hand_on(c, j).wait_send()
 
         pltpu.make_async_copy(grecv.at[parity], grecv.at[parity], g_recv.at[parity]).wait()
-        row = (row + jnp.sum(grecv[parity], axis=0)) / cells
+        row = (gmsg[...] + jnp.sum(grecv[parity], axis=0)) / cells
         pltpu.make_async_copy(grecv.at[parity], grecv.at[parity], g_send).wait()
 
         fresh = [

time: 143 us -> 139 us (0.972)
  Pallas kernels: 139 us -> 135 us
    pallas_call x1, Pallas kernels: 139 us -> 135 us  [local(): pl.pallas_call(kernel, out_shape=(jax.ShapeDtypeStruct((ROWS, D), F32), j...]
where the time goes in v4:
time: 139 us
  Pallas kernels  135 us (97%)
  local copies, waits for them, and re-layouts  2.83 us (2%)
    pallas_call x1, Pallas kernels, local(): pl.pallas_call(kernel, out_shape=(jax.ShapeDtypeStruct((ROWS, D), F32), j...  135 us
    unnamed x2, local copies, waits for them, and re-layouts  2.83 us

profile of v4, /device:TPU:1, one launch (start us, length us, event | category | flops | bytes accessed | tf_op | source)
XLA Modules:
  0.0 138.9 jit_solution(17765808373286615186)
XLA Ops:
  0.6 135.4 %shard_map.68 = (f32[8,4096]{1,0:T(8,128)}, f32[5,5]{1,0:T(8,128)}) custom-call(bf16[8,4096]{1,0:T(8,128)(2,1)} %bitcast.14, f32[1,4096]{1,0:T(1,128)} %gain_ref.1, bf16[344,4096]{1,0:T(8,128)(2,1)} %bitcast.10, bf16[344,4096]{1,0:T(8,128)(2,1)} %bitcast.11, bf16[344,4096]{1,0:T(8,128)(2,1)} %bitcast.12), custom_call_target="tpu_custom_call" | custom-call | tf_op jit(solution)/shard_map/pallas_call | solution.py:444
  136.0 1.3 copy.7
  137.3 1.6 %copy.9 = f32[1,8,4096]{2,1,0:T(8,128)} copy(f32[1,8,4096]{2,1,0:T(8,128)} %bitcast.13) | data formatting | bytes 262144
